TPU v7x, 256 devices: a 2x2x32 block of a 4x8x32 slice. The times are simulated.
256 devices in a mesh: parts: 4 (over y, x), ka: 64 (over z, core).
Axes of the slice: x: 2, y: 2, z: 32, core: 2. Of those that a mesh axis runs over, the one named last changes fastest.
The devices are a block of a 4x8x32 slice.
Arguments:
- energies: float32 [256, 200], P(('parts', 'ka')), parts along dimension 0, may hold values from -4 to 4
- proj: float32 [256, 2, 10, 200], P(('parts', 'ka')), parts along dimension 0, may hold values from -0.3125 to 0.3125
- window: int32 [256, 2], P(('parts', 'ka')), parts along dimension 0, may hold values from 0 to 200, as said below
- sigma: float32 [8, 10, 10, 256], P('parts', None, None, 'ka'), parts along dimension 0, may hold values from -3 to 1.5, as said below
- impurity_inverse: float32 [8, 10, 10, 256], P('parts', None, None, 'ka'), parts along dimension 0, may hold values from -5 to 50, as said below
Outputs:
- density: float32 [256, 2, 200, 200], P(('parts', 'ka')), parts along dimension 0
- sigma_new: float32 [8, 10, 10, 256], P('parts', None, None, 'ka'), parts along dimension 0
There are 4 independent parts, one for each index of `parts`. A program takes and returns all parts, laid end to end along the dimension named above; each array names one. Nothing has to cross between parts.
Inputs may be any that keep to these rules, and one draw needn't show every extreme that they name: window[k, 0] < 40 and window[k, 1] >= 160 for every k-point. For every frequency, sigma[0] and sigma[1] are real symmetric matrices and -sigma[1] is positive definite with smallest eigenvalue 0.2 or more. For every frequency n, impurity_inverse[0] and impurity_inverse[1] are real symmetric matrices and impurity_inverse[1] + sigma[1] - freqs[n] times the identity is positive definite with smallest eigenvalue 0.2 or more.
All inputs are finite; a program needn't handle non-finite values.
Results may differ from a plain program's by a relative error of at most 0.00011.
Values sent between devices are 32-bit elements; how exact they have to be, the bound alone decides.
A program may use at most 64 MiB of HBM per device.

v0:
```python
import math

import jax
import jax.numpy as jnp
from jax import lax
from jax.experimental import pallas as pl
from jax.experimental.pallas import tpu as pltpu
from jax.sharding import PartitionSpec as P

f32 = jnp.float32
bf16 = jnp.bfloat16
HI = lax.Precision.HIGHEST
MESH = pl.DeviceIdType.MESH
inverse_temp = 40.0
SEGS = 4
NO = 10
JP = 16
LN = 128


def tail_weight(count):
    total = 0.0
    for number in range(count):
        total += (inverse_temp / (math.pi * (2 * number + 1))) ** 2
    return inverse_temp / 4.0 - 2.0 / inverse_temp * total


def dot(a, b, ca, cb):
    return lax.dot_general(
        a, b, (((ca,), (cb,)), ((), ())), precision=HI, preferred_element_type=f32
    )


def bdot(a, b):
    return jnp.dot(a, b, preferred_element_type=f32)


def split(x):
    high = x.astype(bf16)
    return high, (x - high.astype(f32)).astype(bf16)


def iota(shape, dim):
    return lax.broadcasted_iota(jnp.int32, shape, dim)


def one_hot(cond):
    return jnp.where(cond, 1.0, 0.0).astype(f32)


def placed(array, line, p):
    pieces = [array[:p]] if p else []
    pieces.append(line)
    if p + 1 < array.shape[0]:
        pieces.append(array[p + 1 :])
    return jnp.concatenate(pieces, axis=0)


def invert(ar, ai):
    cols = iota(ar.shape, 1)
    for p in range(NO):
        pr, pi = ar[p : p + 1, p : p + 1, :], ai[p : p + 1, p : p + 1, :]
        inv = 1.0 / (pr * pr + pi * pi)
        rr, ri = pr * inv, -pi * inv
        rowr, rowi = ar[p : p + 1], ai[p : p + 1]
        at = cols[p : p + 1] == p
        nr = jnp.where(at, rr, rowr * rr - rowi * ri)
        ni = jnp.where(at, ri, rowr * ri + rowi * rr)
        cr, ci = ar[:, p : p + 1, :], ai[:, p : p + 1, :]
        br = jnp.where(cols == p, 0.0, ar)
        bi = jnp.where(cols == p, 0.0, ai)
        br = br - (cr * nr - ci * ni)
        bi = bi - (cr * ni + ci * nr)
        ar, ai = placed(br, nr, p), placed(bi, ni, p)
    return ar, ai


def cmul(ar, ai, br, bi):
    outr = outi = None
    for l in range(NO):
        xr, xi = ar[:, l : l + 1, :], ai[:, l : l + 1, :]
        yr, yi = br[l : l + 1], bi[l : l + 1]
        tr, ti = xr * yr - xi * yi, xr * yi + xi * yr
        outr = tr if outr is None else outr + tr
        outi = ti if outi is None else outi + ti
    return outr, outi


def build(devices, nf, bands):
    near = devices // SEGS
    own = SEGS * nf
    batch = near * own
    bp = (bands + LN - 1) // LN * LN
    rows = (bands + 15) // 16 * 16
    count = devices * nf
    step = near * nf
    per = 4
    groups = near // per
    gn = per * own
    weight = tail_weight(count)
    unit = math.pi / inverse_temp

    def freq_of(slot, place):
        return step * (slot // nf) + nf * place + slot % nf

    def kernel(
        w_ref, e_ref, proj_ref, sig_ref, imp_ref, dens_ref, out_ref,
        p16, pt, e2, sfix, s_all, part, send_a, recv_a, send_x, recv_x, h_src, h_dst,
        lh, ll, rh, rl, cacc,
        as_sem, ar_sem, xs_sem, xr_sem, ss_sem, sr_sem, ps_sem, pr_sem, hs_sem, hr_sem, loc_sem,
    ):
        me = lax.axis_index("ka")
        seg = me // near
        pos = lax.rem(me, near)
        base = seg * near
        up = lax.rem(me + near, devices)
        down = lax.rem(me + devices - near, devices)
        seg_up = lax.rem(seg + 1, SEGS)
        seg_down = lax.rem(seg + SEGS - 1, SEGS)
        seg_far = lax.rem(seg + 2, SEGS)

        def peer(off):
            return lax.rem(pos + off, near)

        barrier = pltpu.get_barrier_semaphore()
        for target in (up, down):
            pl.semaphore_signal(barrier, inc=1, device_id={"ka": target}, device_id_type=MESH)

        def greet(off, _):
            pl.semaphore_signal(
                barrier, inc=1, device_id={"ka": base + peer(off)}, device_id_type=MESH
            )
            return 0

        lax.fori_loop(1, near, greet, 0)

        lane = iota((1, bands), 1)
        inside = jnp.where((lane >= w_ref[0, 0]) & (lane < w_ref[0, 1]), 1.0, 0.0).astype(f32)
        p16[...] = jnp.zeros_like(p16)
        e2[...] = jnp.zeros_like(e2)
        e2[0:1, 0:bands] = e_ref[...]
        for c in range(2):
            for i in range(NO):
                p16[c, i : i + 1, 0:bands] = proj_ref[0, i, c : c + 1, :] * inside
        for kind, ref in enumerate((sig_ref, imp_ref)):
            for c in range(2):
                for i in range(NO):
                    at = 2 * nf * kind + nf * c
                    sfix[i, at : at + nf, :] = ref[c, i]
        packed = None
        for i in range(NO):
            place = one_hot(iota((NO, LN), 1) == NO * i + iota((NO, LN), 0))
            term = dot(sfix[i], place, 1, 0)
            packed = term if packed is None else packed + term
        s_all[seg] = packed

        oh_i = one_hot((iota((JP, LN), 1) // NO == iota((JP, LN), 0)) & (iota((JP, LN), 1) < NO * NO))
        oh_j = one_hot(
            (lax.rem(iota((JP, LN), 1), NO) == iota((JP, LN), 0)) & (iota((JP, LN), 1) < NO * NO)
        )
        pr, pi = p16[0], p16[1]
        pir, pii = dot(pr, oh_i, 0, 0), dot(pi, oh_i, 0, 0)
        pjr, pji = dot(pr, oh_j, 0, 0), dot(pi, oh_j, 0, 0)
        ppr = pir * pjr + pii * pji
        ppi = pii * pjr - pir * pji
        eye = one_hot(iota((JP, JP), 0) == iota((JP, JP), 1))
        pt[0] = dot(pr, eye, 0, 0)
        pt[1] = dot(pi, eye, 0, 0)

        row = iota((near * 2 * own, bp), 0)
        num = freq_of(lax.rem(row, own), row // (2 * own))
        omega = (2.0 * num.astype(f32) + 1.0) * unit
        energy = e2[0:1, :]
        recip = 1.0 / (energy * energy + omega * omega)
        g1, g2 = -energy * recip, -omega * recip
        real_row = lax.rem(row // own, 2) == 0
        a_all = dot(jnp.where(real_row, g1, g2), ppr, 1, 0) + dot(
            jnp.where(real_row, -g2, g1), ppi, 1, 0
        )
        send_a[...] = a_all.reshape(near, 2 * own, LN)

        pl.semaphore_wait(barrier, near + 1)

        def far_copy(buf, index, lo, size, sems, sem, target):
            return pltpu.make_async_remote_copy(
                src_ref=buf.at[index, pl.ds(lo, size), :],
                dst_ref=buf.at[index, pl.ds(lo, size), :],
                send_sem=sems[0].at[sem],
                recv_sem=sems[1].at[sem],
                device_id={"ka": target},
                device_id_type=MESH,
            )

        def far_start(buf, size, sems):
            far_copy(buf, seg, 0, size, sems, 0, up).start()
            far_copy(buf, seg, 0, size, sems, 1, down).start()

        def far_relay(buf, size, sems):
            half = size // 2
            far_copy(buf, seg_down, 0, size, sems, 0, up).wait_recv()
            far_copy(buf, seg_down, 0, half, sems, 2, up).start()
            far_copy(buf, seg_up, 0, size, sems, 1, down).wait_recv()
            far_copy(buf, seg_up, half, half, sems, 3, down).start()

        def far_end(buf, size, sems):
            half = size // 2
            far_copy(buf, seg_far, 0, half, sems, 2, up).wait_recv()
            far_copy(buf, seg_far, half, half, sems, 3, down).wait_recv()
            far_copy(buf, seg, 0, size, sems, 0, up).wait_send()
            far_copy(buf, seg, 0, size, sems, 1, down).wait_send()
            far_copy(buf, seg_down, 0, half, sems, 2, up).wait_send()
            far_copy(buf, seg_up, half, half, sems, 3, down).wait_send()

        def near_copy(src, dst, to, source, sems):
            return pltpu.make_async_remote_copy(
                src_ref=src.at[to],
                dst_ref=dst.at[source],
                send_sem=sems[0].at[to],
                recv_sem=sems[1].at[source],
                device_id={"ka": base + to},
                device_id_type=MESH,
            )

        order = [near // 2]
        for k in range(1, near // 2):
            order += [near // 2 - k, near // 2 + k]

        def near_start(src, dst, sems):
            for off in order:
                near_copy(src, dst, peer(off), pos, sems).start()

        s_sems, p_sems = (ss_sem, sr_sem), (ps_sem, pr_sem)
        a_sems, x_sems = (as_sem, ar_sem), (xs_sem, xr_sem)
        s_rows = 4 * nf
        far_start(s_all, s_rows, s_sems)
        near_start(send_a, recv_a, a_sems)
        recv_a[pos] = send_a[pos]

        e_col = dot(e2[0:1, :], jnp.ones((1, LN), f32), 0, 0)[0:rows]

        def left(g, _):
            ln = iota((rows, LN), 1)
            n64 = lax.rem(ln, gn)
            om = (
                2.0 * freq_of(lax.rem(n64, own), per * g + n64 // own).astype(f32) + 1.0
            ) * unit
            rec = 1.0 / (e_col * e_col + om * om)
            gr, gi = -e_col * rec, -om * rec
            first = ln < gn
            ga = jnp.where(first, gr, -gi)
            gb = jnp.where(first, gi, gr)
            for i in range(NO):
                cr, ci = pt[0, 0:rows, i : i + 1], pt[1, 0:rows, i : i + 1]
                th, tl = split(ga * cr + gb * ci)
                lh[g, 0:rows, LN * i : LN * i + LN] = th
                ll[g, 0:rows, LN * i : LN * i + LN] = tl
                th, tl = split(gb * cr - ga * ci)
                lh[g, rows : 2 * rows, LN * i : LN * i + LN] = th
                ll[g, rows : 2 * rows, LN * i : LN * i + LN] = tl
            return 0

        lax.fori_loop(0, groups // 2, left, 0)
        far_relay(s_all, s_rows, s_sems)
        lax.fori_loop(groups // 2, groups, left, 0)

        sel = one_hot(
            (iota((NO * JP, LN), 1) == NO * (iota((NO * JP, LN), 0) // JP) + lax.rem(iota((NO * JP, LN), 0), JP))
            & (lax.rem(iota((NO * JP, LN), 0), JP) < NO)
        )

        def arrive(dst, sems, source):
            @pl.when(source != pos)
            def _():
                near_copy(dst, dst, source, source, sems).wait_recv()

        def wait_all(dst, sems):
            def one(source, _):
                arrive(dst, sems, source)
                return 0

            lax.fori_loop(0, near, one, 0)

        def sent_all(src, sems):
            def one(off, _):
                near_copy(src, src, peer(off), pos, sems).wait_send()
                return 0

            lax.fori_loop(1, near, one, 0)

        def cube(x):
            return x.reshape(NO, JP, batch)

        def flat(x):
            return x.reshape(NO * JP, batch)

        wait_all(recv_a, a_sems)
        hyb = [
            cube(dot(sel, recv_a[:, c * own : (c + 1) * own, :].reshape(batch, LN), 1, 1))
            for c in range(2)
        ]
        ainv_r, ainv_i = invert(*hyb)

        far_end(s_all, s_rows, s_sems)
        s_flat = dot(sel, s_all[...].reshape(SEGS * s_rows, LN), 1, 1)
        at_row = iota((SEGS * s_rows, batch), 0)
        slot = lax.rem(iota((SEGS * s_rows, batch), 1), own)

        def spread(kind, c):
            hit = (at_row // s_rows == slot // nf) & (
                lax.rem(at_row, s_rows) == 2 * nf * kind + nf * c + lax.rem(slot, nf)
            )
            return dot(s_flat, one_hot(hit), 1, 0)

        sg_r, sg_i = spread(0, 0), spread(0, 1)
        im_r, im_i = spread(1, 0), spread(1, 1)
        gorb = invert(ainv_r - cube(sg_r), ainv_i - cube(sg_i))
        pick = one_hot(lax.rem(iota((own, batch), 1), own) == iota((own, batch), 0))
        sums = [dot(dot(pick, flat(x), 1, 1), sel, 1, 0) for x in gorb]
        part[seg, 0:own, :] = sums[0]
        part[seg, own : 2 * own, :] = sums[1]
        far_start(part, 2 * own, p_sems)
        far_relay(part, 2 * own, p_sems)
        sent_all(send_a, a_sems)
        far_end(part, 2 * own, p_sems)
        total = (part[0] + part[1] + part[2] + part[3]) * (1.0 / devices)
        t_flat = dot(sel, total, 1, 1)
        t_row = iota((2 * own, batch), 0)
        t_slot = lax.rem(iota((2 * own, batch), 1), own)
        loc = [cube(dot(t_flat, one_hot(t_row == t_slot + own * c), 1, 0)) for c in range(2)]
        linv_r, linv_i = invert(*loc)
        d_r, d_i = flat(linv_r) - im_r, flat(linv_i) - im_i
        q0, q1 = iota((NO * JP, NO * JP), 0), iota((NO * JP, NO * JP), 1)
        same = one_hot(q0 == q1)
        turned = one_hot((q0 // JP == lax.rem(q1, JP)) & (lax.rem(q0, JP) == q1 // JP))
        new_r = sg_r + dot(0.5 * (same + turned), d_r, 1, 0)
        new_i = sg_i + dot(0.5 * (same - turned), d_i, 1, 0)

        own_row = iota((8, batch), 0)
        own_lane = iota((8, batch), 1)
        last = one_hot((own_lane == own - 1) & (own_row == 0))
        last_r = dot(dot(last, new_r, 1, 1), sel, 1, 0)
        last_i = dot(dot(last, new_i, 1, 1), sel, 1, 0)
        h_src[...] = last_r + pltpu.roll(last_i, 1, 0)

        def h_copy(off, sem):
            return pltpu.make_async_remote_copy(
                src_ref=h_src,
                dst_ref=h_dst,
                send_sem=hs_sem.at[sem],
                recv_sem=hr_sem,
                device_id={"ka": base + peer(off)},
                device_id_type=MESH,
            )

        @pl.when(pos == near - 1)
        def _():
            for off in range(1, near):
                h_copy(off, off).start()
            keep = pltpu.make_async_copy(h_src, h_dst, loc_sem)
            keep.start()
            keep.wait()

        gnew = invert(ainv_r - cube(new_r), ainv_i - cube(new_i))
        sn = cube(new_r), cube(new_i)
        half = cmul(*sn, *gnew)
        full = cmul(*half, *sn)
        for c in range(2):
            x = dot(flat(sn[c] + full[c]), sel, 0, 0)
            send_x[:, c * own : (c + 1) * own, :] = x.reshape(near, own, LN)
        near_start(send_x, recv_x, x_sems)
        recv_x[pos] = send_x[pos]

        mine_hit = (own_row < nf) & (own_lane == nf * seg + own_row)
        mine = one_hot(mine_hit)
        for c, value in enumerate((new_r, new_i)):
            lines = dot(dot(mine, value, 1, 1), sel, 1, 0)
            for i in range(NO):
                place = one_hot(iota((NO, LN), 1) == NO * i + iota((NO, LN), 0))
                out_ref[c, i] = dot(lines, place, 1, 1)[0:nf]

        @pl.when(pos != near - 1)
        def _():
            h_copy(1, 0).wait_recv()

        def square(line):
            wide = jnp.broadcast_to(line, (JP, LN))
            return dot(wide * oh_i, oh_j, 1, 1), dot(wide * oh_j, oh_i, 1, 1)

        m_r, mt_r = square(h_dst[0:1, :])
        m_i, mt_i = square(h_dst[1:2, :])
        h_r, h_i = 0.5 * (m_r + mt_r), 0.5 * (m_i - mt_i)
        hp_r = dot(h_r, pr, 1, 0) - dot(h_i, pi, 1, 0)
        hp_i = dot(h_r, pi, 1, 0) + dot(h_i, pr, 1, 0)
        ptr, pti = pt[0], pt[1]
        quad_r = dot(ptr, hp_r, 1, 0) + dot(pti, hp_i, 1, 0)
        quad_i = dot(ptr, hp_i, 1, 0) - dot(pti, hp_r, 1, 0)

        pjt_r, pjt_i = dot(oh_j, pr, 0, 0), dot(oh_j, pi, 0, 0)
        wr = split(jnp.concatenate([pjt_r, -pjt_i], axis=0))
        wi = split(jnp.concatenate([pjt_i, pjt_r], axis=0))
        cacc[...] = jnp.zeros_like(cacc)

        def total_of(g, _):
            for t in range(per):
                arrive(recv_x, x_sems, per * g + t)
            block = recv_x[pl.ds(per * g, per), :, :]
            x = jnp.concatenate(
                [block[:, c * own : (c + 1) * own, :].reshape(gn, LN) for c in range(2)], axis=1
            )
            orb = iota((NO, 1, 2 * LN), 0)
            which = lax.rem(iota((NO, 1, 2 * LN), 2), LN) // NO
            xm = jnp.where(which == orb, x[None], 0.0).reshape(NO * gn, 2 * LN)
            xh, xl = split(xm)
            mr = bdot(xh, wr[0]) + bdot(xh, wr[1]) + bdot(xl, wr[0])
            mi = bdot(xh, wi[0]) + bdot(xh, wi[1]) + bdot(xl, wi[0])
            rn = iota((gn, bp), 0)
            om = (
                2.0 * freq_of(lax.rem(rn, own), per * g + rn // own).astype(f32) + 1.0
            ) * unit
            rec = 1.0 / (energy * energy + om * om)
            gr, gi = -energy * rec, -om * rec
            for i in range(NO):
                a, b = mr[gn * i : gn * i + gn], mi[gn * i : gn * i + gn]
                th, tl = split(a * gr - b * gi)
                rh[2 * gn * i : 2 * gn * i + gn, :] = th
                rl[2 * gn * i : 2 * gn * i + gn, :] = tl
                th, tl = split(a * gi + b * gr)
                rh[2 * gn * i + gn : 2 * gn * i + 2 * gn, :] = th
                rl[2 * gn * i + gn : 2 * gn * i + 2 * gn, :] = tl
            cacc[...] += bdot(lh[g], rh[...]) + bdot(lh[g], rl[...]) + bdot(ll[g], rh[...])
            return 0

        lax.fori_loop(0, groups, total_of, 0)
        c_r = jnp.concatenate([cacc[0:bands, :], jnp.zeros((bp - bands, bp), f32)], axis=0)
        c_i = jnp.concatenate([cacc[rows : rows + bands, :], jnp.zeros((bp - bands, bp), f32)], axis=0)
        scale = 1.0 / inverse_temp
        d0 = (c_r + c_r.T) * scale - weight * quad_r
        d1 = (c_i - c_i.T) * scale - weight * quad_i
        dens_ref[0, 0] = d0[0:bands, 0:bands]
        dens_ref[0, 1] = d1[0:bands, 0:bands]

        sent_all(send_x, x_sems)

        @pl.when(pos == near - 1)
        def _():
            for off in range(1, near):
                h_copy(off, off).wait_send()

    dma = pltpu.SemaphoreType.DMA
    return pl.pallas_call(
        kernel,
        out_shape=(
            jax.ShapeDtypeStruct((1, 2, bands, bands), f32),
            jax.ShapeDtypeStruct((2, NO, nf, NO), f32),
        ),
        in_specs=[pl.BlockSpec(memory_space=pltpu.SMEM)]
        + [pl.BlockSpec(memory_space=pltpu.VMEM)] * 4,
        out_specs=(pl.BlockSpec(memory_space=pltpu.VMEM),) * 2,
        scratch_shapes=[
            pltpu.VMEM((2, JP, bp), f32),
            pltpu.VMEM((2, bp, JP), f32),
            pltpu.VMEM((8, bp), f32),
            pltpu.VMEM((NO, 4 * nf, NO), f32),
            pltpu.VMEM((SEGS, 4 * nf, LN), f32),
            pltpu.VMEM((SEGS, 2 * own, LN), f32),
            pltpu.VMEM((near, 2 * own, LN), f32),
            pltpu.VMEM((near, 2 * own, LN), f32),
            pltpu.VMEM((near, 2 * own, LN), f32),
            pltpu.VMEM((near, 2 * own, LN), f32),
            pltpu.VMEM((8, LN), f32),
            pltpu.VMEM((8, LN), f32),
            pltpu.VMEM((groups, 2 * rows, NO * LN), bf16),
            pltpu.VMEM((groups, 2 * rows, NO * LN), bf16),
            pltpu.VMEM((NO * LN, bp), bf16),
            pltpu.VMEM((NO * LN, bp), bf16),
            pltpu.VMEM((2 * rows, bp), f32),
            dma((near,)), dma((near,)), dma((near,)), dma((near,)),
            dma((4,)), dma((4,)), dma((4,)), dma((4,)),
            dma((near,)), dma, dma,
        ],
        compiler_params=pltpu.CompilerParams(
            collective_id=0, has_side_effects=True, vmem_limit_bytes=48 * 1024 * 1024
        ),
        name="charge_update",
    )


def solution(mesh):
    devices = mesh.shape["ka"]

    def local(energies, proj, window, sigma, impurity_inverse):
        call = build(devices, sigma.shape[3], energies.shape[1])
        density, new = call(
            window,
            energies,
            jnp.swapaxes(proj, 1, 2),
            jnp.swapaxes(sigma, 2, 3),
            jnp.swapaxes(impurity_inverse, 2, 3),
        )
        return density, jnp.swapaxes(new, 2, 3)

    both = ("parts", "ka")
    in_specs = (
        P(both, None),
        P(both, None, None, None),
        P(both, None),
        P("parts", None, None, "ka"),
        P("parts", None, None, "ka"),
    )
    out_specs = (P(both, None, None, None), P("parts", None, None, "ka"))
    return jax.shard_map(local, mesh=mesh, in_specs=in_specs, out_specs=out_specs, check_vma=False)
```

profile of v0, /device:TPU:37, one launch (start us, length us, event | category | flops | bytes accessed | tf_op | source)
XLA Modules:
  0.0 90.0 jit_solution(7685191578144131758)
XLA Ops:
  0.6 0.0 copy-start.3
  0.6 0.0 copy-start.4
  0.7 0.7 copy-done.3
  1.3 0.0 copy-done.4
  1.3 0.0 copy-start
  1.3 0.8 copy-done
  2.1 0.0 copy-start.1
  2.1 0.8 copy-done.1
  2.9 0.0 copy-start.2
  2.9 0.7 copy-done.2
  3.6 85.0 %charge_update.1 = (f32[1,2,200,200]{3,2,1,0:T(8,128)S(1)}, f32[2,10,4,10]{3,2,1,0:T(4,128)S(1)}) custom-call(s32[1,2]{1,0:T(1,128)S(1)} %copy-done.4, f32[1,200]{1,0:T(1,128)S(1)} %copy-done.3, f32[1,10,2,200]{3,2,1,0:T(2,128)S(1)} %bitcast.7, f32[2,10,4,10]{3,2,1,0:T(4,128)S(1)} %bitcast.4, f32[2,10,4,10]{3,2,1,0:T(4,128)S(1)} %bitcast.5), custom_call_target="tpu_custom_call" | custom-call | tf_op jit(solution)/shard_map/charge_update/pallas_call | solution.py:493
  88.6 0.8 copy.9
  89.4 0.6 copy.10
Async XLA Ops:
  0.6 0.7 copy-start.3
  0.6 0.7 copy-start.4
  1.3 0.8 copy-start
  2.1 0.8 copy-start.1
  2.9 0.7 copy-start.2
where the time goes:
time: 90.3 us; the launch traced here: 90 us
  Pallas kernels  85 us (94%)
  local copies, waits for them, and re-layouts  4.32 us (5%)
    pallas_call x1, Pallas kernels, local(): call(window, energies, jnp.swapaxes(proj, 1, 2), jnp.swapaxes(sigma, 2, 3...  85 us
    unnamed x12, local copies, waits for them, and re-layouts  4.32 us

commit v1 on v0

--- a/solution.py
+++ b/solution.py
@@ -98,16 +98,19 @@
     groups = near // per
     gn = per * own
     weight = tail_weight(count)
+    dense = 2 * own * NO * NO // LN
+    cut = 2 * own
     unit = math.pi / inverse_temp
 
     def freq_of(slot, place):
         return step * (slot // nf) + nf * place + slot % nf
 
     def kernel(
-        w_ref, e_ref, proj_ref, sig_ref, imp_ref, dens_ref, out_ref,
-        p16, pt, e2, sfix, s_all, part, send_a, recv_a, send_x, recv_x, h_src, h_dst,
+        w_hbm, e_hbm, proj_hbm, sig_hbm, imp_hbm, dens_ref, out_ref,
+        w_ref, e_ref, proj_ref, sig_ref, imp_ref,
+        p16, pt, e2, sfix, gsr, gsi, masks, s_all, part, send_a, recv_a, send_x, recv_x, h_src, h_dst,
         lh, ll, rh, rl, cacc,
-        as_sem, ar_sem, xs_sem, xr_sem, ss_sem, sr_sem, ps_sem, pr_sem, hs_sem, hr_sem, loc_sem,
+        as_sem, ar_sem, xs_sem, xr_sem, ss_sem, sr_sem, ps_sem, pr_sem, hs_sem, hr_sem, loc_sem, in_sem,
     ):
         me = lax.axis_index("ka")
         seg = me // near
@@ -122,6 +125,16 @@
         def peer(off):
             return lax.rem(pos + off, near)
 
+        sources = (e_hbm, proj_hbm, w_hbm, sig_hbm, imp_hbm)
+        targets = (e_ref, proj_ref, w_ref, sig_ref, imp_ref)
+        loads = [
+            pltpu.make_async_copy(a, b, in_sem.at[k])
+            for k, (a, b) in enumerate(zip(sources, targets))
+        ]
+        for load in loads:
+            load.start()
+        recv_a[:, dense - 1 : 2 * own, :] = jnp.zeros((near, 2 * own - dense + 1, LN), f32)
+
         barrier = pltpu.get_barrier_semaphore()
         for target in (up, down):
             pl.semaphore_signal(barrier, inc=1, device_id={"ka": target}, device_id_type=MESH)
@@ -134,10 +147,13 @@
 
         lax.fori_loop(1, near, greet, 0)
 
-        lane = iota((1, bands), 1)
-        inside = jnp.where((lane >= w_ref[0, 0]) & (lane < w_ref[0, 1]), 1.0, 0.0).astype(f32)
         p16[...] = jnp.zeros_like(p16)
         e2[...] = jnp.zeros_like(e2)
+        sfix[...] = jnp.zeros_like(sfix)
+        for load in loads:
+            load.wait()
+        lane = iota((1, bands), 1)
+        inside = one_hot((lane >= w_ref[0:1, 0:1]) & (lane < w_ref[0:1, 1:2]))
         e2[0:1, 0:bands] = e_ref[...]
         for c in range(2):
             for i in range(NO):
@@ -146,11 +162,10 @@
             for c in range(2):
                 for i in range(NO):
                     at = 2 * nf * kind + nf * c
-                    sfix[i, at : at + nf, :] = ref[c, i]
+                    sfix[i, at : at + nf, 0:NO] = ref[c, i]
         packed = None
         for i in range(NO):
-            place = one_hot(iota((NO, LN), 1) == NO * i + iota((NO, LN), 0))
-            term = dot(sfix[i], place, 1, 0)
+            term = pltpu.roll(sfix[i], NO * i, 1) if i else sfix[i]
             packed = term if packed is None else packed + term
         s_all[seg] = packed
 
@@ -159,25 +174,39 @@
             (lax.rem(iota((JP, LN), 1), NO) == iota((JP, LN), 0)) & (iota((JP, LN), 1) < NO * NO)
         )
         pr, pi = p16[0], p16[1]
-        pir, pii = dot(pr, oh_i, 0, 0), dot(pi, oh_i, 0, 0)
-        pjr, pji = dot(pr, oh_j, 0, 0), dot(pi, oh_j, 0, 0)
-        ppr = pir * pjr + pii * pji
-        ppi = pii * pjr - pir * pji
         eye = one_hot(iota((JP, JP), 0) == iota((JP, JP), 1))
         pt[0] = dot(pr, eye, 0, 0)
         pt[1] = dot(pi, eye, 0, 0)
 
-        row = iota((near * 2 * own, bp), 0)
-        num = freq_of(lax.rem(row, own), row // (2 * own))
+        dr = iota((LN, JP), 0)
+        di = dense * (dr // cut) + lax.rem(dr, cut)
+        real = lax.rem(dr, cut) < dense
+        ex_i = one_hot((di // NO == iota((LN, JP), 1)) & real)
+        ex_j = one_hot((lax.rem(di, NO) == iota((LN, JP), 1)) & real)
+        pir, pii = dot(ex_i, pr, 1, 0), dot(ex_i, pi, 1, 0)
+        pjr, pji = dot(ex_j, pr, 1, 0), dot(ex_j, pi, 1, 0)
+        ppr = pir * pjr + pii * pji
+        ppi = pii * pjr - pir * pji
+        row = iota((near * cut, bp), 0)
+        num = freq_of(lax.rem(row, own), row // cut)
         omega = (2.0 * num.astype(f32) + 1.0) * unit
         energy = e2[0:1, :]
         recip = 1.0 / (energy * energy + omega * omega)
         g1, g2 = -energy * recip, -omega * recip
         real_row = lax.rem(row // own, 2) == 0
-        a_all = dot(jnp.where(real_row, g1, g2), ppr, 1, 0) + dot(
-            jnp.where(real_row, -g2, g1), ppi, 1, 0
+        a_all = dot(ppr, jnp.where(real_row, g1, g2), 1, 1) + dot(
+            ppi, jnp.where(real_row, -g2, g1), 1, 1
         )
-        send_a[...] = a_all.reshape(near, 2 * own, LN)
+        quarter = iota((cut, LN), 1) // cut
+        for far_place in range(near // 4):
+            for place in range(4):
+                block = None
+                for q in range(4):
+                    piece = a_all[cut * q : cut * q + cut, LN * far_place : LN * far_place + LN]
+                    turn = (cut * (q - place)) % LN
+                    piece = pltpu.roll(piece, turn, 1) if turn else piece
+                    block = piece if block is None else jnp.where(quarter == q, piece, block)
+                send_a[4 * far_place + place] = block
 
         pl.semaphore_wait(barrier, near + 1)
 
@@ -211,39 +240,50 @@
             far_copy(buf, seg_down, 0, half, sems, 2, up).wait_send()
             far_copy(buf, seg_up, half, half, sems, 3, down).wait_send()
 
-        def near_copy(src, dst, to, source, sems):
+        def near_copy(src, dst, to, source, sems, size):
             return pltpu.make_async_remote_copy(
-                src_ref=src.at[to],
-                dst_ref=dst.at[source],
+                src_ref=src.at[to, pl.ds(0, size), :],
+                dst_ref=dst.at[source, pl.ds(0, size), :],
                 send_sem=sems[0].at[to],
                 recv_sem=sems[1].at[source],
                 device_id={"ka": base + to},
                 device_id_type=MESH,
             )
 
-        order = [near // 2]
-        for k in range(1, near // 2):
-            order += [near // 2 - k, near // 2 + k]
-
-        def near_start(src, dst, sems):
-            for off in order:
-                near_copy(src, dst, peer(off), pos, sems).start()
+        def at_turn(turn):
+            return lax.rem(
+                pos + near + near // 2 + (turn + 1) // 2 * (1 - 2 * lax.rem(turn, 2)), near
+            )
+
+        def near_start(src, dst, sems, size):
+            for turn in range(near - 1):
+                off = near // 2 + (turn + 1) // 2 * (1 - 2 * (turn % 2))
+                near_copy(src, dst, peer(off), pos, sems, size).start()
 
         s_sems, p_sems = (ss_sem, sr_sem), (ps_sem, pr_sem)
         a_sems, x_sems = (as_sem, ar_sem), (xs_sem, xr_sem)
         s_rows = 4 * nf
         far_start(s_all, s_rows, s_sems)
-        near_start(send_a, recv_a, a_sems)
+        near_start(send_a, recv_a, a_sems, dense)
         recv_a[pos] = send_a[pos]
+        orb = iota((NO, gn, 2 * LN), 0)
+        which = lax.rem(iota((NO, gn, 2 * LN), 2), LN) // NO
+        masks[...] = one_hot(which == orb).astype(bf16)
 
         e_col = dot(e2[0:1, :], jnp.ones((1, LN), f32), 0, 0)[0:rows]
 
+        def omega_of(number, g):
+            place = at_turn(per * g + number // own)
+            return (2.0 * freq_of(lax.rem(number, own), place).astype(f32) + 1.0) * unit
+
         def left(g, _):
+            om = omega_of(iota((gn, bp), 0), g)
+            rec = 1.0 / (energy * energy + om * om)
+            gsr[g] = -energy * rec
+            gsi[g] = -om * rec
             ln = iota((rows, LN), 1)
             n64 = lax.rem(ln, gn)
-            om = (
-                2.0 * freq_of(lax.rem(n64, own), per * g + n64 // own).astype(f32) + 1.0
-            ) * unit
+            om = omega_of(n64, g)
             rec = 1.0 / (e_col * e_col + om * om)
             gr, gi = -e_col * rec, -om * rec
             first = ln < gn
@@ -268,21 +308,21 @@
             & (lax.rem(iota((NO * JP, LN), 0), JP) < NO)
         )
 
-        def arrive(dst, sems, source):
+        def arrive(dst, sems, source, size):
             @pl.when(source != pos)
             def _():
-                near_copy(dst, dst, source, source, sems).wait_recv()
-
-        def wait_all(dst, sems):
+                near_copy(dst, dst, source, source, sems, size).wait_recv()
+
+        def wait_all(dst, sems, size):
             def one(source, _):
-                arrive(dst, sems, source)
+                arrive(dst, sems, source, size)
                 return 0
 
             lax.fori_loop(0, near, one, 0)
 
-        def sent_all(src, sems):
+        def sent_all(src, sems, size):
             def one(off, _):
-                near_copy(src, src, peer(off), pos, sems).wait_send()
+                near_copy(src, src, peer(off), pos, sems, size).wait_send()
                 return 0
 
             lax.fori_loop(1, near, one, 0)
@@ -293,12 +333,32 @@
         def flat(x):
             return x.reshape(NO * JP, batch)
 
-        wait_all(recv_a, a_sems)
-        hyb = [
-            cube(dot(sel, recv_a[:, c * own : (c + 1) * own, :].reshape(batch, LN), 1, 1))
-            for c in range(2)
-        ]
-        ainv_r, ainv_i = invert(*hyb)
+        sr = iota((NO * JP, LN), 0)
+        sc = iota((NO * JP, LN), 1)
+        to_cube = one_hot(
+            (dense * (sc // cut) + lax.rem(sc, cut) == NO * (sr // JP) + lax.rem(sr, JP))
+            & (lax.rem(sr, JP) < NO)
+            & (lax.rem(sc, cut) < dense)
+        )
+        eighth = iota((cut, LN), 1) // own
+
+        def gathered(c):
+            lines = []
+            for q in range(4):
+                halves = []
+                for far_k in range(near // 8):
+                    block = None
+                    for k in range(8):
+                        piece = recv_a[8 * far_k + k]
+                        turn = (own * k - cut * q - own * c) % LN
+                        piece = pltpu.roll(piece, turn, 1) if turn else piece
+                        block = piece if block is None else jnp.where(eighth == k, piece, block)
+                    halves.append(block)
+                lines.append(jnp.concatenate(halves, axis=1))
+            return cube(dot(to_cube, jnp.concatenate(lines, axis=0), 1, 0))
+
+        wait_all(recv_a, a_sems, dense)
+        ainv_r, ainv_i = invert(gathered(0), gathered(1))
 
         far_end(s_all, s_rows, s_sems)
         s_flat = dot(sel, s_all[...].reshape(SEGS * s_rows, LN), 1, 1)
@@ -318,10 +378,16 @@
         sums = [dot(dot(pick, flat(x), 1, 1), sel, 1, 0) for x in gorb]
         part[seg, 0:own, :] = sums[0]
         part[seg, own : 2 * own, :] = sums[1]
-        far_start(part, 2 * own, p_sems)
-        far_relay(part, 2 * own, p_sems)
-        sent_all(send_a, a_sems)
-        far_end(part, 2 * own, p_sems)
+        far = lax.rem(me + 2 * near, devices)
+        far_copy(part, seg, 0, cut, p_sems, 2, far).start()
+        far_start(part, cut, p_sems)
+        sent_all(send_a, a_sems, dense)
+        far_copy(part, seg_down, 0, cut, p_sems, 0, up).wait_recv()
+        far_copy(part, seg_up, 0, cut, p_sems, 1, down).wait_recv()
+        far_copy(part, seg_far, 0, cut, p_sems, 2, far).wait_recv()
+        far_copy(part, seg, 0, cut, p_sems, 0, up).wait_send()
+        far_copy(part, seg, 0, cut, p_sems, 1, down).wait_send()
+        far_copy(part, seg, 0, cut, p_sems, 2, far).wait_send()
         total = (part[0] + part[1] + part[2] + part[3]) * (1.0 / devices)
         t_flat = dot(sel, total, 1, 1)
         t_row = iota((2 * own, batch), 0)
@@ -352,6 +418,16 @@
                 device_id_type=MESH,
             )
 
+        gnew = invert(ainv_r - cube(new_r), ainv_i - cube(new_i))
+        sn = cube(new_r), cube(new_i)
+        half = cmul(*sn, *gnew)
+        full = cmul(*half, *sn)
+        for c in range(2):
+            x = dot(flat(sn[c] + full[c]), sel, 0, 0)
+            send_x[:, c * own : (c + 1) * own, :] = x.reshape(near, own, LN)
+        near_start(send_x, recv_x, x_sems, cut)
+        recv_x[pos] = send_x[pos]
+
         @pl.when(pos == near - 1)
         def _():
             for off in range(1, near):
@@ -360,16 +436,6 @@
             keep.start()
             keep.wait()
 
-        gnew = invert(ainv_r - cube(new_r), ainv_i - cube(new_i))
-        sn = cube(new_r), cube(new_i)
-        half = cmul(*sn, *gnew)
-        full = cmul(*half, *sn)
-        for c in range(2):
-            x = dot(flat(sn[c] + full[c]), sel, 0, 0)
-            send_x[:, c * own : (c + 1) * own, :] = x.reshape(near, own, LN)
-        near_start(send_x, recv_x, x_sems)
-        recv_x[pos] = send_x[pos]
-
         mine_hit = (own_row < nf) & (own_lane == nf * seg + own_row)
         mine = one_hot(mine_hit)
         for c, value in enumerate((new_r, new_i)):
@@ -378,47 +444,29 @@
                 place = one_hot(iota((NO, LN), 1) == NO * i + iota((NO, LN), 0))
                 out_ref[c, i] = dot(lines, place, 1, 1)[0:nf]
 
-        @pl.when(pos != near - 1)
-        def _():
-            h_copy(1, 0).wait_recv()
-
-        def square(line):
-            wide = jnp.broadcast_to(line, (JP, LN))
-            return dot(wide * oh_i, oh_j, 1, 1), dot(wide * oh_j, oh_i, 1, 1)
-
-        m_r, mt_r = square(h_dst[0:1, :])
-        m_i, mt_i = square(h_dst[1:2, :])
-        h_r, h_i = 0.5 * (m_r + mt_r), 0.5 * (m_i - mt_i)
-        hp_r = dot(h_r, pr, 1, 0) - dot(h_i, pi, 1, 0)
-        hp_i = dot(h_r, pi, 1, 0) + dot(h_i, pr, 1, 0)
-        ptr, pti = pt[0], pt[1]
-        quad_r = dot(ptr, hp_r, 1, 0) + dot(pti, hp_i, 1, 0)
-        quad_i = dot(ptr, hp_i, 1, 0) - dot(pti, hp_r, 1, 0)
-
         pjt_r, pjt_i = dot(oh_j, pr, 0, 0), dot(oh_j, pi, 0, 0)
         wr = split(jnp.concatenate([pjt_r, -pjt_i], axis=0))
         wi = split(jnp.concatenate([pjt_i, pjt_r], axis=0))
         cacc[...] = jnp.zeros_like(cacc)
 
         def total_of(g, _):
-            for t in range(per):
-                arrive(recv_x, x_sems, per * g + t)
-            block = recv_x[pl.ds(per * g, per), :, :]
+            places = [at_turn(per * g + t) for t in range(per)]
+            for place in places:
+                arrive(recv_x, x_sems, place, cut)
+            blocks = [recv_x[place] for place in places]
             x = jnp.concatenate(
-                [block[:, c * own : (c + 1) * own, :].reshape(gn, LN) for c in range(2)], axis=1
-            )
-            orb = iota((NO, 1, 2 * LN), 0)
-            which = lax.rem(iota((NO, 1, 2 * LN), 2), LN) // NO
-            xm = jnp.where(which == orb, x[None], 0.0).reshape(NO * gn, 2 * LN)
-            xh, xl = split(xm)
+                [
+                    jnp.concatenate([b[c * own : (c + 1) * own] for b in blocks], axis=0)
+                    for c in range(2)
+                ],
+                axis=1,
+            )
+            xh, xl = split(x)
+            xh = (xh[None] * masks[...]).reshape(NO * gn, 2 * LN)
+            xl = (xl[None] * masks[...]).reshape(NO * gn, 2 * LN)
             mr = bdot(xh, wr[0]) + bdot(xh, wr[1]) + bdot(xl, wr[0])
             mi = bdot(xh, wi[0]) + bdot(xh, wi[1]) + bdot(xl, wi[0])
-            rn = iota((gn, bp), 0)
-            om = (
-                2.0 * freq_of(lax.rem(rn, own), per * g + rn // own).astype(f32) + 1.0
-            ) * unit
-            rec = 1.0 / (energy * energy + om * om)
-            gr, gi = -energy * rec, -om * rec
+            gr, gi = gsr[g], gsi[g]
             for i in range(NO):
                 a, b = mr[gn * i : gn * i + gn], mi[gn * i : gn * i + gn]
                 th, tl = split(a * gr - b * gi)
@@ -430,7 +478,26 @@
             cacc[...] += bdot(lh[g], rh[...]) + bdot(lh[g], rl[...]) + bdot(ll[g], rh[...])
             return 0
 
-        lax.fori_loop(0, groups, total_of, 0)
+        lax.fori_loop(0, groups - 1, total_of, 0)
+
+        @pl.when(pos != near - 1)
+        def _():
+            h_copy(1, 0).wait_recv()
+
+        def square(line):
+            wide = jnp.broadcast_to(line, (JP, LN))
+            return dot(wide * oh_i, oh_j, 1, 1), dot(wide * oh_j, oh_i, 1, 1)
+
+        m_r, mt_r = square(h_dst[0:1, :])
+        m_i, mt_i = square(h_dst[1:2, :])
+        h_r, h_i = 0.5 * (m_r + mt_r), 0.5 * (m_i - mt_i)
+        hp_r = dot(h_r, pr, 1, 0) - dot(h_i, pi, 1, 0)
+        hp_i = dot(h_r, pi, 1, 0) + dot(h_i, pr, 1, 0)
+        ptr, pti = pt[0], pt[1]
+        quad_r = dot(ptr, hp_r, 1, 0) + dot(pti, hp_i, 1, 0)
+        quad_i = dot(ptr, hp_i, 1, 0) - dot(pti, hp_r, 1, 0)
+
+        lax.fori_loop(groups - 1, groups, total_of, 0)
         c_r = jnp.concatenate([cacc[0:bands, :], jnp.zeros((bp - bands, bp), f32)], axis=0)
         c_i = jnp.concatenate([cacc[rows : rows + bands, :], jnp.zeros((bp - bands, bp), f32)], axis=0)
         scale = 1.0 / inverse_temp
@@ -439,7 +506,7 @@
         dens_ref[0, 0] = d0[0:bands, 0:bands]
         dens_ref[0, 1] = d1[0:bands, 0:bands]
 
-        sent_all(send_x, x_sems)
+        sent_all(send_x, x_sems, cut)
 
         @pl.when(pos == near - 1)
         def _():
@@ -453,14 +520,21 @@
             jax.ShapeDtypeStruct((1, 2, bands, bands), f32),
             jax.ShapeDtypeStruct((2, NO, nf, NO), f32),
         ),
-        in_specs=[pl.BlockSpec(memory_space=pltpu.SMEM)]
-        + [pl.BlockSpec(memory_space=pltpu.VMEM)] * 4,
+        in_specs=[pl.BlockSpec(memory_space=pltpu.HBM)] * 5,
         out_specs=(pl.BlockSpec(memory_space=pltpu.VMEM),) * 2,
         scratch_shapes=[
+            pltpu.VMEM((1, 2), jnp.int32),
+            pltpu.VMEM((1, bands), f32),
+            pltpu.VMEM((1, NO, 2, bands), f32),
+            pltpu.VMEM((2, NO, nf, NO), f32),
+            pltpu.VMEM((2, NO, nf, NO), f32),
             pltpu.VMEM((2, JP, bp), f32),
             pltpu.VMEM((2, bp, JP), f32),
             pltpu.VMEM((8, bp), f32),
-            pltpu.VMEM((NO, 4 * nf, NO), f32),
+            pltpu.VMEM((NO, 4 * nf, LN), f32),
+            pltpu.VMEM((groups, gn, bp), f32),
+            pltpu.VMEM((groups, gn, bp), f32),
+            pltpu.VMEM((NO, gn, 2 * LN), bf16),
             pltpu.VMEM((SEGS, 4 * nf, LN), f32),
             pltpu.VMEM((SEGS, 2 * own, LN), f32),
             pltpu.VMEM((near, 2 * own, LN), f32),
@@ -476,10 +550,10 @@
             pltpu.VMEM((2 * rows, bp), f32),
             dma((near,)), dma((near,)), dma((near,)), dma((near,)),
             dma((4,)), dma((4,)), dma((4,)), dma((4,)),
-            dma((near,)), dma, dma,
+            dma((near,)), dma, dma, dma((5,)),
         ],
         compiler_params=pltpu.CompilerParams(
-            collective_id=0, has_side_effects=True, vmem_limit_bytes=48 * 1024 * 1024
+            collective_id=0, has_side_effects=True, vmem_limit_bytes=67043328
         ),
         name="charge_update",
     )

time: 90.3 us -> 87.5 us (0.969)
  local copies, waits for them, and re-layouts: 4.32 us -> 2.41 us
    unnamed x12 -> x4, local copies, waits for them, and re-layouts: 4.32 us -> 2.41 us
where the time goes in v1:
time: 87.5 us; the launch traced here: 87.3 us
  Pallas kernels  84.2 us (96%)
  local copies, waits for them, and re-layouts  2.41 us (3%)
    pallas_call x1, Pallas kernels, local(): call(window, energies, jnp.swapaxes(proj, 1, 2), jnp.swapaxes(sigma, 2, 3...  84.2 us
    unnamed x4, local copies, waits for them, and re-layouts  2.41 us

profile of v1, /device:TPU:37, one launch (start us, length us, event | category | flops | bytes accessed | tf_op | source)
XLA Modules:
  0.0 87.3 jit_solution(7641139276603775926)
XLA Ops:
  0.6 84.2 %charge_update.1 = (f32[1,2,200,200]{3,2,1,0:T(8,128)}, f32[2,10,4,10]{3,2,1,0:T(4,128)}) custom-call(s32[1,2]{1,0:T(1,128)} %w_hbm.1, f32[1,200]{1,0:T(1,128)} %e_hbm.1, f32[1,10,2,200]{3,2,1,0:T(2,128)} %bitcast.7, f32[2,10,4,10]{3,2,1,0:T(4,128)} %bitcast.4, f32[2,10,4,10]{3,2,1,0:T(4,128)} %bitcast.5), custom_call_target="tpu_custom_call" | custom-call | tf_op jit(solution)/shard_map/charge_update/pallas_call | solution.py:567
  84.9 0.0 copy-start
  84.9 1.8 %copy.9 = f32[1,2,200,200]{3,2,1,0:T(8,128)} copy(f32[1,2,200,200]{3,2,1,0:T(8,128)} %get-tuple-element.8) | data formatting | bytes 640000
  86.7 0.0 copy-done
  86.7 0.6 copy.10
Async XLA Ops:
  84.9 1.8 %copy-start = (f32[2,10,4,10]{3,2,1,0:T(4,128)S(1)}, f32[2,10,4,10]{3,2,1,0:T(4,128)}, u32[]{:S(2)}) copy-start(f32[2,10,4,10]{3,2,1,0:T(4,128)} %get-tuple-element.5) | copy-start | bytes 9604

commit v2 on v1

--- a/solution.py
+++ b/solution.py
@@ -109,7 +109,7 @@
         w_hbm, e_hbm, proj_hbm, sig_hbm, imp_hbm, dens_ref, out_ref,
         w_ref, e_ref, proj_ref, sig_ref, imp_ref,
         p16, pt, e2, sfix, gsr, gsi, masks, s_all, part, send_a, recv_a, send_x, recv_x, h_src, h_dst,
-        lh, ll, rh, rl, cacc,
+        lcat, rcat, wcat, cacc,
         as_sem, ar_sem, xs_sem, xr_sem, ss_sem, sr_sem, ps_sem, pr_sem, hs_sem, hr_sem, loc_sem, in_sem,
     ):
         me = lax.axis_index("ka")
@@ -291,12 +291,11 @@
             gb = jnp.where(first, gi, gr)
             for i in range(NO):
                 cr, ci = pt[0, 0:rows, i : i + 1], pt[1, 0:rows, i : i + 1]
-                th, tl = split(ga * cr + gb * ci)
-                lh[g, 0:rows, LN * i : LN * i + LN] = th
-                ll[g, 0:rows, LN * i : LN * i + LN] = tl
-                th, tl = split(gb * cr - ga * ci)
-                lh[g, rows : 2 * rows, LN * i : LN * i + LN] = th
-                ll[g, rows : 2 * rows, LN * i : LN * i + LN] = tl
+                for half, value in enumerate((ga * cr + gb * ci, gb * cr - ga * ci)):
+                    th, tl = split(value)
+                    for part_k, piece in enumerate((th, th, tl)):
+                        at = LN * (NO * part_k + i)
+                        lcat[g, rows * half : rows * half + rows, at : at + LN] = piece
             return 0
 
         lax.fori_loop(0, groups // 2, left, 0)
@@ -425,9 +424,6 @@
         for c in range(2):
             x = dot(flat(sn[c] + full[c]), sel, 0, 0)
             send_x[:, c * own : (c + 1) * own, :] = x.reshape(near, own, LN)
-        near_start(send_x, recv_x, x_sems, cut)
-        recv_x[pos] = send_x[pos]
-
         @pl.when(pos == near - 1)
         def _():
             for off in range(1, near):
@@ -436,6 +432,9 @@
             keep.start()
             keep.wait()
 
+        near_start(send_x, recv_x, x_sems, cut)
+        recv_x[pos] = send_x[pos]
+
         mine_hit = (own_row < nf) & (own_lane == nf * seg + own_row)
         mine = one_hot(mine_hit)
         for c, value in enumerate((new_r, new_i)):
@@ -445,15 +444,29 @@
                 out_ref[c, i] = dot(lines, place, 1, 1)[0:nf]
 
         pjt_r, pjt_i = dot(oh_j, pr, 0, 0), dot(oh_j, pi, 0, 0)
-        wr = split(jnp.concatenate([pjt_r, -pjt_i], axis=0))
-        wi = split(jnp.concatenate([pjt_i, pjt_r], axis=0))
+        wide = jnp.concatenate(
+            [
+                jnp.concatenate([pjt_r, -pjt_i], axis=0),
+                jnp.concatenate([pjt_i, pjt_r], axis=0),
+            ],
+            axis=1,
+        )
+        w_high, w_low = split(wide)
+        for k, piece in enumerate((w_high, w_low, w_high)):
+            wcat[2 * LN * k : 2 * LN * k + 2 * LN, :] = piece
         cacc[...] = jnp.zeros_like(cacc)
 
-        def total_of(g, _):
-            places = [at_turn(per * g + t) for t in range(per)]
-            for place in places:
-                arrive(recv_x, x_sems, place, cut)
-            blocks = [recv_x[place] for place in places]
+        def offset(turn):
+            return near // 2 + (turn + 1) // 2 * (1 - 2 * (turn % 2))
+
+        def wait_group(g):
+            for turn in range(per * g, per * g + per):
+                if offset(turn) % near:
+                    source = peer(offset(turn))
+                    near_copy(recv_x, recv_x, source, source, x_sems, cut).wait_recv()
+
+        def right(g):
+            blocks = [recv_x[peer(offset(turn))] for turn in range(per * g, per * g + per)]
             x = jnp.concatenate(
                 [
                     jnp.concatenate([b[c * own : (c + 1) * own] for b in blocks], axis=0)
@@ -464,40 +477,47 @@
             xh, xl = split(x)
             xh = (xh[None] * masks[...]).reshape(NO * gn, 2 * LN)
             xl = (xl[None] * masks[...]).reshape(NO * gn, 2 * LN)
-            mr = bdot(xh, wr[0]) + bdot(xh, wr[1]) + bdot(xl, wr[0])
-            mi = bdot(xh, wi[0]) + bdot(xh, wi[1]) + bdot(xl, wi[0])
+            mixed = bdot(jnp.concatenate([xh, xh, xl], axis=1), wcat[...])
             gr, gi = gsr[g], gsi[g]
+            slot_r = g % 2
             for i in range(NO):
-                a, b = mr[gn * i : gn * i + gn], mi[gn * i : gn * i + gn]
-                th, tl = split(a * gr - b * gi)
-                rh[2 * gn * i : 2 * gn * i + gn, :] = th
-                rl[2 * gn * i : 2 * gn * i + gn, :] = tl
-                th, tl = split(a * gi + b * gr)
-                rh[2 * gn * i + gn : 2 * gn * i + 2 * gn, :] = th
-                rl[2 * gn * i + gn : 2 * gn * i + 2 * gn, :] = tl
-            cacc[...] += bdot(lh[g], rh[...]) + bdot(lh[g], rl[...]) + bdot(ll[g], rh[...])
-            return 0
-
-        lax.fori_loop(0, groups - 1, total_of, 0)
-
-        @pl.when(pos != near - 1)
-        def _():
-            h_copy(1, 0).wait_recv()
-
-        def square(line):
-            wide = jnp.broadcast_to(line, (JP, LN))
-            return dot(wide * oh_i, oh_j, 1, 1), dot(wide * oh_j, oh_i, 1, 1)
-
-        m_r, mt_r = square(h_dst[0:1, :])
-        m_i, mt_i = square(h_dst[1:2, :])
-        h_r, h_i = 0.5 * (m_r + mt_r), 0.5 * (m_i - mt_i)
-        hp_r = dot(h_r, pr, 1, 0) - dot(h_i, pi, 1, 0)
-        hp_i = dot(h_r, pi, 1, 0) + dot(h_i, pr, 1, 0)
-        ptr, pti = pt[0], pt[1]
-        quad_r = dot(ptr, hp_r, 1, 0) + dot(pti, hp_i, 1, 0)
-        quad_i = dot(ptr, hp_i, 1, 0) - dot(pti, hp_r, 1, 0)
-
-        lax.fori_loop(groups - 1, groups, total_of, 0)
+                a, b = mixed[gn * i : gn * i + gn, 0:bp], mixed[gn * i : gn * i + gn, bp : 2 * bp]
+                for c, value in enumerate((a * gr - b * gi, a * gi + b * gr)):
+                    th, tl = split(value)
+                    for k, piece in enumerate((th, tl, th)):
+                        at = NO * LN * k + LN * i + gn * c
+                        rcat[slot_r, at : at + gn, :] = piece
+
+        def total_of(g):
+            cacc[...] += bdot(lcat[g], rcat[g % 2])
+
+        def tail():
+            def square(line):
+                wide = jnp.broadcast_to(line, (JP, LN))
+                return dot(wide * oh_i, oh_j, 1, 1), dot(wide * oh_j, oh_i, 1, 1)
+
+            m_r, mt_r = square(h_dst[0:1, :])
+            m_i, mt_i = square(h_dst[1:2, :])
+            h_r, h_i = 0.5 * (m_r + mt_r), 0.5 * (m_i - mt_i)
+            hp_r = dot(h_r, pr, 1, 0) - dot(h_i, pi, 1, 0)
+            hp_i = dot(h_r, pi, 1, 0) + dot(h_i, pr, 1, 0)
+            ptr, pti = pt[0], pt[1]
+            quad_r = dot(ptr, hp_r, 1, 0) + dot(pti, hp_i, 1, 0)
+            quad_i = dot(ptr, hp_i, 1, 0) - dot(pti, hp_r, 1, 0)
+            return quad_r, quad_i
+
+        for g in range(groups):
+            wait_group(g)
+            if g == 1:
+                @pl.when(pos != near - 1)
+                def _():
+                    h_copy(1, 0).wait_recv()
+
+                quad_r, quad_i = tail()
+            right(g)
+            if g:
+                total_of(g - 1)
+        total_of(groups - 1)
         c_r = jnp.concatenate([cacc[0:bands, :], jnp.zeros((bp - bands, bp), f32)], axis=0)
         c_i = jnp.concatenate([cacc[rows : rows + bands, :], jnp.zeros((bp - bands, bp), f32)], axis=0)
         scale = 1.0 / inverse_temp
@@ -543,10 +563,9 @@
             pltpu.VMEM((near, 2 * own, LN), f32),
             pltpu.VMEM((8, LN), f32),
             pltpu.VMEM((8, LN), f32),
-            pltpu.VMEM((groups, 2 * rows, NO * LN), bf16),
-            pltpu.VMEM((groups, 2 * rows, NO * LN), bf16),
-            pltpu.VMEM((NO * LN, bp), bf16),
-            pltpu.VMEM((NO * LN, bp), bf16),
+            pltpu.VMEM((groups, 2 * rows, 3 * NO * LN), bf16),
+            pltpu.VMEM((2, 3 * NO * LN, bp), bf16),
+            pltpu.VMEM((6 * LN, 2 * bp), bf16),
             pltpu.VMEM((2 * rows, bp), f32),
             dma((near,)), dma((near,)), dma((near,)), dma((near,)),
             dma((4,)), dma((4,)), dma((4,)), dma((4,)),

time: 87.5 us -> 87.1 us (level)
  no operation moved by 1% of the time
where the time goes in v2:
time: 87.1 us; the launch traced here: 86.9 us
  Pallas kernels  83.8 us (96%)
  local copies, waits for them, and re-layouts  2.41 us (3%)
    pallas_call x1, Pallas kernels, local(): call(window, energies, jnp.swapaxes(proj, 1, 2), jnp.swapaxes(sigma, 2, 3...  83.8 us
    unnamed x4, local copies, waits for them, and re-layouts  2.41 us

profile of v2, /device:TPU:37, one launch (start us, length us, event | category | flops | bytes accessed | tf_op | source)
XLA Modules:
  0.0 86.9 jit_solution(13472258441203765102)
XLA Ops:
  0.6 83.8 %charge_update.1 = (f32[1,2,200,200]{3,2,1,0:T(8,128)}, f32[2,10,4,10]{3,2,1,0:T(4,128)}) custom-call(s32[1,2]{1,0:T(1,128)} %w_hbm.1, f32[1,200]{1,0:T(1,128)} %e_hbm.1, f32[1,10,2,200]{3,2,1,0:T(2,128)} %bitcast.7, f32[2,10,4,10]{3,2,1,0:T(4,128)} %bitcast.4, f32[2,10,4,10]{3,2,1,0:T(4,128)} %bitcast.5), custom_call_target="tpu_custom_call" | custom-call | tf_op jit(solution)/shard_map/charge_update/pallas_call | solution.py:586
  84.5 0.0 copy-start
  84.5 1.8 %copy.9 = f32[1,2,200,200]{3,2,1,0:T(8,128)} copy(f32[1,2,200,200]{3,2,1,0:T(8,128)} %get-tuple-element.8) | data formatting | bytes 640000
  86.3 0.0 copy-done
  86.3 0.6 copy.10
Async XLA Ops:
  84.5 1.8 %copy-start = (f32[2,10,4,10]{3,2,1,0:T(4,128)S(1)}, f32[2,10,4,10]{3,2,1,0:T(4,128)}, u32[]{:S(2)}) copy-start(f32[2,10,4,10]{3,2,1,0:T(4,128)} %get-tuple-element.5) | copy-start | bytes 9604
